TPU v7x, 16 devices: a whole 2x2x2 slice. The times are simulated.
16 devices in a mesh: yy: 2 (over z), zz: 2 (over y), t: 4 (over x, core).
Axes of the slice: x: 2, y: 2, z: 2, core: 2. Of those that a mesh axis runs over, the one named last changes fastest.
Arguments:
- fat_links: float32 [4, 24, 128, 8, 24, 3, 3, 2], P(None, 't', 'zz', 'yy')
- long_links: float32 [4, 24, 128, 8, 24, 3, 3, 2], P(None, 't', 'zz', 'yy')
- source: float32 [24, 128, 8, 12, 3, 2], P('t', 'zz', 'yy')
- quark_mass: float32 [1], replicated
Outputs:
- output 1: float32 [24, 128, 8, 12, 3, 2], P('t', 'zz', 'yy')
- output 2: float32 [8], replicated
All inputs are finite; a program needn't handle non-finite values.
Results may differ from a plain program's by a relative error of at most 0.001.
Values are sent between devices in bfloat16 or wider.
A program may use at most 1 GiB of HBM per device.

v0:
```python
import jax
import jax.numpy as jnp
from jax import lax
from jax.experimental import pallas as pl
from jax.experimental.pallas import tpu as pltpu
from jax.sharding import PartitionSpec as P

MESH = pl.DeviceIdType.MESH
ITERS = 8
ROWS = 72
NV = 9
EXT = 152
F32 = jnp.float32


SUB, LANES, HALF = 8, 128, 64
BASE = 40
MATS = 18
XH = 12
STRIDE = 36
DEVS = 16
NEAR, FAR = 1, 3
PP = (2, 2)
CUTS = ('t', 'zz', 'yy')
COLS = 6


TF1, TF3, TB1, TB3, ZF1, ZF3, ZB1, ZB3, LS, LO, RS, RO, X0, XP, XM, X2 = range(16)


def flip(bit):
    return 1 - bit


def out_slot_of(mu, typ, yp):
    return {0: TF1 + typ, 1: ZF1 + typ, 2: (LS + (RO - LS) * yp, RO - yp)[typ]}[mu]


def rows8(i):
    return pl.ds(pl.multiple_of(i * SUB, SUB), SUB)


def swap_halves(v):
    return pltpu.roll(v, LANES // 2, 1)


def cg_kernel(src_ref, mass_ref, fat_ref, long_ref, sol_ref, norm_ref,
              g, fx, fy, zs, zr, pv, xv, wv, xh_i, pz_i, red_own, red, scal,
              st, dn, y_out, y_in, tv_in, tw_in, zl_out, zl_in,
              st_sem, ly_send, ly_recv, lt_send, lt_recv, lz_send, lz_recv,
              send_sem, recv_sem, rsend_sem, rrecv_sem):
    yy = lax.axis_index('yy')
    zz = lax.axis_index('zz')
    tt = lax.axis_index('t')
    me = yy * SUB + zz * 4 + tt

    raw = (fat_ref, long_ref)

    def raw_copies(mu, blk, slot):
        return [pltpu.make_async_copy(raw[typ].at[mu, blk // 2, blk % 2 + 2 * h], st.at[slot, typ, h], st_sem.at[slot, typ, h]) for typ in range(2) for h in range(2)]

    MUS = (2, 0, 1, 3)
    for cp in raw_copies(MUS[0], 0, 0):
        cp.start()

    lane = lax.broadcasted_iota(jnp.int32, (SUB, LANES), 1)
    sub = lax.broadcasted_iota(jnp.int32, (SUB, LANES), 0)
    zlane = lane % HALF
    zslot = ((lane + 3) % HALF) // SUB
    half1 = lane >= HALF

    def masks(i, carry):
        row = sub + i * SUB
        t_row = row // XH
        xh_i[rows8(i), :] = row - t_row * XH
        pz_i[rows8(i), :] = (t_row + zlane) % 2
        return carry
    lax.fori_loop(0, NV, masks, 0)

    def halo_copies(fi, c):
        def mk(src, dst, kind, dev):
            return pltpu.make_async_remote_copy(src_ref=src, dst_ref=dst, send_sem=send_sem.at[fi, c, kind], recv_sem=recv_sem.at[fi, c, kind], device_id=dev, device_id_type=MESH)
        return [
            mk(fx.at[fi, c, :, pl.ds(BASE, ROWS), :], fy.at[fi, c], 0, (flip(yy), zz, tt)),
            mk(fx.at[fi, c, :, pl.ds(BASE, BASE), :], fx.at[fi, c, :, pl.ds(112, BASE), :], 1, (yy, zz, (tt + 3) % 4)),
            mk(fx.at[fi, c, :, pl.ds(ROWS, BASE), :], fx.at[fi, c, :, pl.ds(0, BASE), :], 2, (yy, zz, (tt + 1) % 4)),
            mk(zs.at[fi, c], zr.at[fi, c], 3, (yy, flip(zz), tt)),
        ]

    def start_halo(fi, c):
        for cp in halo_copies(fi, c):
            cp.start()

    def wait_send(fi, c):
        for cp in halo_copies(fi, c):
            cp.wait_send()

    def wait_recv(fi, c):
        for cp in halo_copies(fi, c):
            cp.wait_recv()

    def red_copy(slot, d, src_dev):
        dev = ((yy + d // SUB) % 2, (zz + (d // 4) % 2) % 2, (tt + d % 4) % 4)
        return pltpu.make_async_remote_copy(src_ref=red_own.at[slot], dst_ref=red.at[slot, src_dev], send_sem=rsend_sem.at[slot, d], recv_sem=rrecv_sem.at[slot, d], device_id=dev, device_id_type=MESH)

    def red_start(slot, acc):
        red_own[slot] = acc
        for d in range(1, 16):
            red_copy(slot, d, me).start()

    def red_finish(slot):
        for d in range(1, 16):
            src_dev = ((yy + d // SUB) % 2) * SUB + ((zz + (d // 4) % 2) % 2) * 4 + (tt + 4 - d % 4) % 4
            cp = red_copy(slot, d, src_dev)
            cp.wait_send()
            cp.wait_recv()
        red[slot, me] = red_own[slot]
        total = red[slot, 0]
        for d in range(1, 16):
            total = total + red[slot, d]
        total = jnp.sum(jnp.sum(total, axis=0, keepdims=True), axis=1, keepdims=True)
        return jnp.broadcast_to(total, (SUB, LANES))

    def hop_rows(par, c, i):
        fi = flip(par)
        row = pl.multiple_of(i * SUB, SUB)
        acc_re = [None] * 3
        acc_im = [None] * 3

        def term(slot, vec):
            base = slot * MATS
            for a in range(3):
                for b in range(3):
                    l_re = g[par, c, base + a * COLS + b * 2, pl.ds(row, SUB), :]
                    l_im = g[par, c, base + a * COLS + b * 2 + 1, pl.ds(row, SUB), :]
                    t_re = l_re * vec[2 * b] - l_im * vec[2 * b + 1]
                    t_im = l_re * vec[2 * b + 1] + l_im * vec[2 * b]
                    acc_re[a] = t_re if acc_re[a] is None else acc_re[a] + t_re
                    acc_im[a] = t_im if acc_im[a] is None else acc_im[a] + t_im

        def ext(off):
            return [fx[fi, c, k, pl.ds(row + (BASE + off), SUB), :] for k in range(COLS)]

        own = [fx[fi, c, k, pl.ds(row + BASE, SUB), :] for k in range(COLS)]
        xh = xh_i[pl.ds(row, SUB), :]
        x_even = (pz_i[pl.ds(row, SUB), :] + c + yy) % 2 == par
        term(X0, own)
        lo, hi = ext(1), ext(-11)
        term(XP, [jnp.where(xh == 11, h, l) for l, h in zip(lo, hi)])
        lo, hi = ext(-1), ext(11)
        term(XM, [jnp.where(xh == 0, h, l) for l, h in zip(lo, hi)])
        m2, m2w, p2, p2w = ext(-2), ext(10), ext(2), ext(-10)
        term(X2, [jnp.where(x_even, jnp.where(xh < 2, bw, bm), jnp.where(xh > 9, fw, fp)) for bm, bw, fp, fw in zip(m2, m2w, p2, p2w)])
        loc = [fx[fi, flip(c), k, pl.ds(row + BASE, SUB), :] for k in range(COLS)]
        term(LS, loc)
        term(LO, [pltpu.roll(v, HALF, 1) for v in loc])
        zpack = zr[fi, c, pl.ds(row, SUB), :]
        for slot, k in ((ZF1, NEAR), (ZF3, FAR)):
            term(slot, [jnp.where(zlane >= HALF - k, pltpu.roll(zpack, (HALF - k - SUB * j) % LANES, 1), pltpu.roll(own[j], LANES - k, 1)) for j in range(COLS)])
        for slot, k in ((ZB1, NEAR), (ZB3, FAR)):
            term(slot, [jnp.where(zlane < k, pltpu.roll(zpack, (k + HALF - SUB * j) % LANES, 1), pltpu.roll(own[j], k, 1)) for j in range(COLS)])
        term(TF1, ext(XH))
        term(TF3, ext(FAR * XH))
        term(TB1, ext(-XH))
        term(TB3, ext(-FAR * XH))
        rem = [fy[fi, c, k, pl.ds(row, SUB), :] for k in range(COLS)]
        term(RS, rem)
        term(RO, [pltpu.roll(v, HALF, 1) for v in rem])
        return [v for a in range(3) for v in (acc_re[a], acc_im[a])]

    def hop(par, c):
        def body(i, carry):
            out = hop_rows(par, c, i)
            for k in range(COLS):
                wv[k, rows8(i), :] = out[k]
            return carry
        lax.fori_loop(0, NV, body, 0)

    def zpack_of(vals):
        packed = vals[0]
        for j in range(1, COLS):
            packed = jnp.where(zslot == j, pltpu.roll(vals[j], SUB * j, 1), packed)
        return packed

    mass = jnp.full((SUB, LANES), mass_ref[0], F32)
    mass_sq = mass * mass
    zero = jnp.zeros((SUB, LANES), F32)

    def split_src(blk, carry):
        t, yp = blk // 2, blk % 2
        c = (yp + yy) % 2
        for i in range(9):
            dn[0, SUB * i:SUB * i + SUB, :] = jnp.concatenate([src_ref[t, yp, SUB * i:SUB * i + SUB, :], src_ref[t, yp + 2, SUB * i:SUB * i + SUB, :]], axis=1)
        for k in range(COLS):
            fx[0, c, k, pl.ds(t * XH + BASE, SUB), :] = dn[0, pl.ds(k, SUB, stride=COLS), :]
            fx[0, c, k, pl.ds(t * XH + 48, 4), :] = dn[0, pl.ds(k + 48, 4, stride=COLS), :]
        return carry
    lax.fori_loop(0, XH, split_src, 0)

    def init_group(c, acc):
        def body(i, acc):
            row = pl.multiple_of(i * SUB, SUB)
            vals = [fx[0, c, k, pl.ds(row + BASE, SUB), :] for k in range(COLS)]
            for k in range(COLS):
                fx[1, c, k, pl.ds(row + BASE, SUB), :] = zero
                pv[c, k, pl.ds(row, SUB), :] = zero
                xv[c, k, pl.ds(row, SUB), :] = zero
                acc = acc + vals[k] * vals[k]
            zs[0, c, pl.ds(row, SUB), :] = zpack_of(vals)
            return acc
        acc = lax.fori_loop(0, NV, body, acc)
        start_halo(0, c)
        return acc
    acc = lax.fori_loop(0, 2, init_group, zero)
    red_start(1, acc)

    c0, c1 = yy, flip(yy)
    sign = (-1.0, 1.0)
    comps = [(a * COLS + b * 2 + ri, b * COLS + a * 2 + ri, ri) for a in range(3) for b in range(3) for ri in range(2)]

    def mat(par, c, slot, comp, rows):
        return g[par, c, slot * MATS + comp, rows, :]

    def densify(slot, wrap):
        def body(i, carry):
            for u in range(27):
                row = pl.multiple_of(i * (27 * SUB) + u * SUB, SUB)
                for typ in range(2):
                    dn[typ, pl.ds(row + ROWS, SUB), :] = jnp.concatenate([st[slot, typ, 0, pl.ds(row, SUB), :], st[slot, typ, 1, pl.ds(row, SUB), :]], axis=1)
            return carry
        lax.fori_loop(0, 2, body, 0)
        if wrap:
            for typ in range(2):
                dn[typ, :ROWS, :] = dn[typ, COLS * ROWS:, :]

    def compact(order):
        mu = MUS[order]

        def block(blk, carry):
            slot = blk % 2
            t, yp = blk // 2, blk % 2
            c = (yp + yy) % 2

            @pl.when(blk < 11)
            def _():
                for cp in raw_copies(mu, blk + 1, flip(slot)):
                    cp.start()
            if order < 3:
                @pl.when(blk == 11)
                def _():
                    for cp in raw_copies(MUS[order + 1], 0, flip(slot)):
                        cp.start()
            for cp in raw_copies(mu, blk, slot):
                cp.wait()
            densify(slot, mu == 3)
            for off, n in ((0, SUB), (SUB, 4)):
                even = (t + yp + zlane[:n]) % 2 == 0

                def piece(typ, xpar, comp, back=0):
                    return dn[typ, pl.ds(ROWS + xpar * MATS + comp + STRIDE * (off - back), n, stride=STRIDE), :]

                def put(out_slot, comp, par, val):
                    g[par, c, out_slot * MATS + comp, pl.ds(t * XH + off, n), :] = val
                for comp, adj, ri in comps:
                    if mu != 3:
                        for typ in range(2):
                            out_slot = out_slot_of(mu, typ, yp)
                            e, o = piece(typ, 0, comp), piece(typ, 1, comp)
                            put(out_slot, comp, 0, jnp.where(even, e, o))
                            put(out_slot, comp, 1, jnp.where(even, o, e))
                    else:
                        pairs = (
                            (X0, piece(0, 0, comp), sign[ri] * piece(0, 0, adj)),
                            (XP, piece(1, 0, comp), piece(0, 1, comp)),
                            (XM, sign[ri] * piece(0, 1, adj, 1), sign[ri] * piece(1, 0, adj, 1)),
                            (X2, sign[ri] * piece(1, 1, adj, 2), piece(1, 1, comp)),
                        )
                        for out_slot, e, o in pairs:
                            put(out_slot, comp, 0, jnp.where(even, e, o))
                            put(out_slot, comp, 1, jnp.where(even, o, e))
            return carry
        lax.fori_loop(0, XH, block, 0)

    def ly_copies(par):
        dev = (flip(yy), zz, tt)
        return [
            pltpu.make_async_remote_copy(src_ref=g.at[flip(par), c1, pl.ds(RS * MATS, MATS)], dst_ref=g.at[par, c1, pl.ds(RS * MATS, MATS)], send_sem=ly_send.at[par, 0], recv_sem=ly_recv.at[par, 0], device_id=dev, device_id_type=MESH),
            pltpu.make_async_remote_copy(src_ref=y_out.at[par], dst_ref=y_in.at[par], send_sem=ly_send.at[par, 1], recv_sem=ly_recv.at[par, 1], device_id=dev, device_id_type=MESH),
        ]

    def ly_arrivals(par):
        dev = (flip(yy), zz, tt)
        return [
            pltpu.make_async_remote_copy(src_ref=g.at[flip(par), c1, pl.ds(RS * MATS, MATS)], dst_ref=g.at[par, c0, pl.ds(RS * MATS, MATS)], send_sem=ly_send.at[par, 0], recv_sem=ly_recv.at[par, 0], device_id=dev, device_id_type=MESH),
            pltpu.make_async_remote_copy(src_ref=y_out.at[par], dst_ref=y_in.at[par], send_sem=ly_send.at[par, 1], recv_sem=ly_recv.at[par, 1], device_id=dev, device_id_type=MESH),
        ]

    def lt_copies():
        dev = (yy, zz, (tt + 1) % 4)
        out = []
        for par in range(2):
            for c in range(2):
                out.append(pltpu.make_async_remote_copy(src_ref=g.at[flip(par), c, pl.ds(0, MATS), pl.ds(56, 16), :], dst_ref=tv_in.at[par, c], send_sem=lt_send.at[par, c, 0], recv_sem=lt_recv.at[par, c, 0], device_id=dev, device_id_type=MESH))
                out.append(pltpu.make_async_remote_copy(src_ref=g.at[flip(par), c, pl.ds(MATS, MATS), pl.ds(32, BASE), :], dst_ref=tw_in.at[par, c], send_sem=lt_send.at[par, c, 1], recv_sem=lt_recv.at[par, c, 1], device_id=dev, device_id_type=MESH))
        return out

    def lz_copy():
        return pltpu.make_async_remote_copy(src_ref=zl_out, dst_ref=zl_in, send_sem=lz_send, recv_sem=lz_recv, device_id=(yy, flip(zz), tt), device_id_type=MESH)

    compact(0)
    for par in (1, 0):
        def y_pack(i, carry):
            rows = rows8(i)
            v1 = [swap_halves(mat(flip(par), c1, RO, comp, rows)) for comp in range(MATS)]
            for comp in range(MATS):
                y_out[par, comp, rows, :] = jnp.where(half1, mat(flip(par), c0, RO, comp, rows), v1[comp])
            return carry
        lax.fori_loop(0, NV, y_pack, 0)
        for cp in ly_copies(par):
            cp.start()

    compact(1)
    for cp in lt_copies():
        cp.start()

    compact(2)

    def z_pack(n, carry):
        par, c = n // 2, n % 2

        def body(i, carry):
            rows = rows8(i)
            for typ in range(2):
                for third in range(3):
                    zl_out[par, c, typ, third, rows, :] = zpack_of([g[flip(par), c, (4 + typ) * MATS + third * COLS + j, rows, :] for j in range(COLS)])
            return carry
        lax.fori_loop(0, NV, body, 0)
        return carry
    lax.fori_loop(0, 4, z_pack, 0)
    lz_copy().start()

    compact(3)

    for par in (1, 0):
        def y_local(i, carry):
            rows = rows8(i)
            for src_c, own_c in ((c1, c0), (c0, c1)):
                far = [swap_halves(mat(flip(par), src_c, RO, adj, rows)) for comp, adj, ri in comps]
                own = [mat(par, own_c, RO, comp, rows) for comp in range(MATS)]
                for comp, adj, ri in comps:
                    g[par, own_c, LO * MATS + comp, rows, :] = jnp.where(half1, sign[ri] * far[comp], own[comp])
            v0 = [mat(flip(par), c0, LS, adj, rows) for comp, adj, ri in comps]
            for comp, adj, ri in comps:
                g[par, c1, LS * MATS + comp, rows, :] = sign[ri] * v0[comp]
            return carry
        lax.fori_loop(0, NV, y_local, 0)

    for cp in lt_copies():
        cp.wait_send()
        cp.wait_recv()

    def t_back(n, carry):
        par, c = n // 2, n % 2

        def move(slot, dst, load, src):
            for off, cnt in ((0, SUB), (SUB, 4)):
                for comp, adj, ri in comps:
                    g[par, c, slot * MATS + comp, pl.ds(dst + off, cnt), :] = sign[ri] * load(adj, pl.ds(src + off, cnt))

        def v_local(q, carry):
            move(TB1, XH * q + XH, lambda k, rows: g[flip(par), c, k, rows, :], XH * q)
            return carry
        lax.fori_loop(0, 5, v_local, 0)
        move(TB1, 0, lambda k, rows: tv_in[par, c, k, rows, :], 4)

        def w_all(q, carry):
            move(TB3, XH * q + STRIDE, lambda k, rows: g[flip(par), c, MATS + k, rows, :], XH * q)
            move(TB3, XH * q, lambda k, rows: tw_in[par, c, k, rows, :], XH * q + 4)
            return carry
        lax.fori_loop(0, 3, w_all, 0)
        return carry
    lax.fori_loop(0, 4, t_back, 0)

    lz_copy().wait_send()
    lz_copy().wait_recv()

    def z_back(n, carry):
        par, c = n // 2, n % 2

        def body(i, carry):
            rows = rows8(i)
            for typ, k in ((0, NEAR), (1, FAR)):
                packs = [zl_in[par, c, typ, third, rows, :] for third in range(3)]
                back = []
                for comp, adj, ri in comps:
                    own = pltpu.roll(mat(flip(par), c, 4 + typ, adj, rows), k, 1)
                    far = pltpu.roll(packs[adj // COLS], (k + HALF - SUB * (adj % COLS)) % LANES, 1)
                    back.append(sign[ri] * jnp.where(zlane < k, far, own))
                for comp, val in enumerate(back):
                    g[par, c, (COLS + typ) * MATS + comp, rows, :] = val
            return carry
        lax.fori_loop(0, NV, body, 0)
        return carry
    lax.fori_loop(0, 4, z_back, 0)

    for par in (1, 0):
        for cp in ly_copies(par):
            cp.wait_send()
    for par in (1, 0):
        for cp in ly_arrivals(par):
            cp.wait_recv()

        def y_far(i, carry):
            rows = rows8(i)
            w1 = [mat(par, c0, RS, comp, rows) for comp in range(MATS)]
            for comp, adj, ri in comps:
                g[par, c0, RS * MATS + comp, rows, :] = sign[ri] * w1[adj]
            far = [sign[ri] * y_in[par, adj, rows, :] for comp, adj, ri in comps]
            swapped = [swap_halves(v) for v in far]
            for c, vals in ((c0, far), (c1, swapped)):
                own = [mat(par, c, RO, comp, rows) for comp in range(MATS)]
                for comp in range(MATS):
                    g[par, c, RO * MATS + comp, rows, :] = jnp.where(half1, own[comp], vals[comp])
            return carry
        lax.fori_loop(0, NV, y_far, 0)

    rho0 = red_finish(1)
    scal[0] = rho0
    scal[1] = rho0
    scal[2] = zero

    def cg_step(step, carry):
        def odd_group(c, acc):
            wait_recv(0, c)
            hop(1, c)

            @pl.when(step > 0)
            def _():
                wait_send(1, c)

            @pl.when((step > 0) & (c == 0))
            def _():
                rho = red_finish(1)
                norm_ref[pl.ds(step - 1, 1), :] = (rho / scal[0])[0:1]
                scal[2] = rho / scal[1]
                scal[1] = rho
            beta = scal[2]

            def body(n, acc):
                packs = []
                for u in range(3):
                    rows, ext = rows8(n * 3 + u), rows8(n * 3 + u + 5)
                    vals = []
                    for k in range(COLS):
                        s_new = wv[k, rows, :] + beta * fx[1, c, k, ext, :]
                        p_new = fx[0, c, k, ext, :] + beta * pv[c, k, rows, :]
                        fx[1, c, k, ext, :] = s_new
                        pv[c, k, rows, :] = p_new
                        acc = acc + (s_new * s_new + mass_sq * (p_new * p_new))
                        vals.append(s_new)
                    packs.append((rows, zpack_of(vals)))
                for rows, pack in packs:
                    zs[1, c, rows, :] = pack
                return acc
            acc = lax.fori_loop(0, 3, body, acc)

            @pl.when(c == 1)
            def _():
                red_start(0, acc)
            start_halo(1, c)
            return acc
        lax.fori_loop(0, 2, odd_group, zero)

        def even_group(c, acc):
            wait_recv(1, c)
            hop(0, c)
            wait_send(0, c)

            @pl.when(c == 0)
            def _():
                scal[3] = scal[1] / red_finish(0)
            alpha = scal[3]

            def body(n, acc):
                packs = []
                for u in range(3):
                    rows, ext = rows8(n * 3 + u), rows8(n * 3 + u + 5)
                    vals = []
                    for k in range(COLS):
                        p_val = pv[c, k, rows, :]
                        q_val = mass_sq * p_val - wv[k, rows, :]
                        xv[c, k, rows, :] = xv[c, k, rows, :] + alpha * p_val
                        r_new = fx[0, c, k, ext, :] - alpha * q_val
                        fx[0, c, k, ext, :] = r_new
                        acc = acc + r_new * r_new
                        vals.append(r_new)
                    packs.append((rows, zpack_of(vals)))
                for rows, pack in packs:
                    zs[0, c, rows, :] = pack
                return acc
            acc = lax.fori_loop(0, 3, body, acc)

            @pl.when(c == 1)
            def _():
                red_start(1, acc)

            @pl.when(step < ITERS - 1)
            def _():
                start_halo(0, c)
            return acc
        lax.fori_loop(0, 2, even_group, zero)
        return carry
    lax.fori_loop(0, ITERS, cg_step, 0)
    rho = red_finish(1)
    norm_ref[pl.ds(ITERS - 1, 1), :] = (rho / scal[0])[0:1]

    def drain(c, carry):
        wait_send(1, c)
        return carry
    lax.fori_loop(0, 2, drain, 0)

    def join_sol(blk, carry):
        t, yp = blk // 2, blk % 2
        c = (yp + yy) % 2
        for k in range(COLS):
            dn[0, pl.ds(k, SUB, stride=COLS), :] = xv[c, k, pl.ds(t * XH, SUB), :]
            dn[0, pl.ds(k + 48, 4, stride=COLS), :] = xv[c, k, pl.ds(t * XH + SUB, 4), :]
        for i in range(9):
            val = dn[0, SUB * i:SUB * i + SUB, :]
            sol_ref[t, yp, SUB * i:SUB * i + SUB, :] = val[:, :HALF]
            sol_ref[t, yp + 2, SUB * i:SUB * i + SUB, :] = pltpu.roll(val, HALF, 1)[:, :HALF]
        return carry
    lax.fori_loop(0, XH, join_sol, 0)


def solution(mesh):
    link_spec = P(None, *CUTS)
    field_spec = P(*CUTS)
    vmem = pl.BlockSpec(memory_space=pltpu.VMEM)

    def local_solve(fat_links, long_links, source, quark_mass):
        t_len, z_len, y_len, xh_len = source.shape[:4]

        def link_rows(links):
            return jnp.moveaxis(links, 2, -1).reshape(4, t_len, y_len, STRIDE * xh_len, z_len)
        src = jnp.moveaxis(source, 1, -1).reshape(t_len, y_len, COLS * xh_len, z_len)
        hbm = pl.BlockSpec(memory_space=pl.ANY)
        dma = pltpu.SemaphoreType.DMA
        sol, norms = pl.pallas_call(
            cg_kernel,
            out_shape=(jax.ShapeDtypeStruct(src.shape, F32), jax.ShapeDtypeStruct((SUB, LANES), F32)),
            in_specs=[vmem, pl.BlockSpec(memory_space=pltpu.SMEM), hbm, hbm],
            out_specs=(vmem, vmem),
            scratch_shapes=[
                pltpu.VMEM(PP + (288, ROWS, LANES), F32),
                pltpu.VMEM(PP + (COLS, EXT, LANES), F32),
                pltpu.VMEM(PP + (COLS, ROWS, LANES), F32),
                pltpu.VMEM(PP + (ROWS, LANES), F32),
                pltpu.VMEM(PP + (ROWS, LANES), F32),
                pltpu.VMEM((2, COLS, ROWS, LANES), F32),
                pltpu.VMEM((2, COLS, ROWS, LANES), F32),
                pltpu.VMEM((COLS, ROWS, LANES), F32),
                pltpu.VMEM((ROWS, LANES), jnp.int32),
                pltpu.VMEM((ROWS, LANES), jnp.int32),
                pltpu.VMEM((2, SUB, LANES), F32),
                pltpu.VMEM((2, 16, SUB, LANES), F32),
                pltpu.VMEM((4, SUB, LANES), F32),
                pltpu.VMEM(PP + (2, STRIDE * xh_len, z_len), F32),
                pltpu.VMEM((2, 504, LANES), F32),
                pltpu.VMEM((2, MATS, ROWS, LANES), F32),
                pltpu.VMEM((2, MATS, ROWS, LANES), F32),
                pltpu.VMEM(PP + (MATS, 16, LANES), F32),
                pltpu.VMEM(PP + (MATS, BASE, LANES), F32),
                pltpu.VMEM(PP + (2, 3, ROWS, LANES), F32),
                pltpu.VMEM(PP + (2, 3, ROWS, LANES), F32),
                *[dma(PP + n) for n in ((2,), (), (), (2,), (2,))], dma, dma,
                dma(PP + (4,)), dma(PP + (4,)), dma((2, DEVS)), dma((2, DEVS)),
            ],
            compiler_params=pltpu.CompilerParams(has_side_effects=True, vmem_limit_bytes=61 * 1024 * 1024),
        )(src, quark_mass, link_rows(fat_links), link_rows(long_links))
        sol = jnp.moveaxis(sol.reshape(t_len, y_len, xh_len, 3, 2, z_len), -1, 1)
        return sol, norms[:, 0]

    return jax.shard_map(local_solve, mesh=mesh, in_specs=(link_spec, link_spec, field_spec, P()), out_specs=(field_spec, P()), check_vma=False)
```

profile of v0, /device:TPU:0, one launch (start us, length us, event | category | flops | bytes accessed | tf_op | source)
XLA Modules:
  0.0 250.6 jit_solution(15680708860631707489)
XLA Ops:
  1.3 245.6 %shard_map.59 = (f32[6,4,72,64]{3,2,1,0:T(8,128)}, f32[8,128]{1,0:T(8,128)}) custom-call(f32[6,4,72,64]{3,2,1,0:T(8,128)} %bitcast.14, f32[1]{0:T(128)S(6)} %copy.7.mass_ref, f32[4,6,4,432,64]{4,3,2,1,0:T(8,128)} %bitcast.12, f32[4,6,4,432,64]{4,3,2,1,0:T(8,128)} %bitcast.13), custom_call_target="tpu_custom_call" | custom-call | tf_op jit(solution)/shard_map/pallas_call | solution.py:549
  246.9 1.3 slice_reduce_fusion
  248.2 2.4 copy.8
where the time goes:
time: 252 us; the launch traced here: 251 us
  Pallas kernels  246 us (98%)
  local copies, waits for them, and re-layouts  3.69 us (1%)
    pallas_call x1, Pallas kernels, local_solve(): pl.pallas_call(cg_kernel, out_shape=(jax.ShapeDtypeStruct(src.shape, F32)...  246 us

commit v1 on v0

v1 whole, which is shorter than its diff:
```python
import jax
import jax.numpy as jnp
from jax import lax
from jax.experimental import pallas as pl
from jax.experimental.pallas import tpu as pltpu
from jax.sharding import PartitionSpec as P

MESH = pl.DeviceIdType.MESH
ITERS = 8
ROWS = 72
NV = 9
EXT = 152
F32 = jnp.float32


SUB, LANES, HALF = 8, 128, 64
BASE = 40
MATS = 18
XH = 12
STRIDE = 36
DEVS = 16
NEAR, FAR = 1, 3
SLOTS = 4
PP = (2, 2)
CUTS = ('t', 'zz', 'yy')
COLS = 6


TF1, TF3, TB1, TB3, ZF1, ZF3, ZB1, ZB3, LS, LO, RS, RO, X0, XP, XM, X2 = range(16)


def flip(bit):
    return 1 - bit


def out_slot_of(mu, typ, yp):
    return {0: TF1 + typ, 1: ZF1 + typ, 2: (LS + (RO - LS) * yp, RO - yp)[typ]}[mu]


def blk_t(blk):
    return blk // 2 if isinstance(blk, int) else half_of(blk)


def blk_y(blk):
    return blk % 2 if isinstance(blk, int) else mod(blk, 2)


def mod(a, n):
    return lax.rem(a, jnp.full_like(a, n))


def half_of(a):
    return lax.div(a, jnp.full_like(a, 2))


def rows8(i):
    return pl.ds(pl.multiple_of(i * SUB, SUB), SUB)


def swap_halves(v):
    return pltpu.roll(v, LANES // 2, 1)


def cg_kernel(src_ref, mass_ref, fat_ref, long_ref, sol_ref, norm_ref,
              g, fx, fy, zs, zr, pv, xv, wv, xh_i, pz_i, red_own, red, scal,
              st, dn, pw, y_out, y_in, tv_in, tw_in, zl_out, zl_in,
              st_sem, ly_send, ly_recv, lt_send, lt_recv, lz_send, lz_recv,
              send_sem, recv_sem, rsend_sem, rrecv_sem):
    yy = lax.axis_index('yy')
    zz = lax.axis_index('zz')
    tt = lax.axis_index('t')
    t_prev, t_next = mod(tt + 3, 4), mod(tt + 1, 4)
    me = yy * SUB + zz * 4 + tt

    raw = (fat_ref, long_ref)

    def raw_copies(mu, blk, slot):
        return [pltpu.make_async_copy(raw[typ].at[mu, blk_t(blk), blk_y(blk) + 2 * h], st.at[slot, typ, h], st_sem.at[slot, typ, h]) for typ in range(2) for h in range(2)]

    MUS = (2, 0, 1, 3)
    for ahead in range(SLOTS - 1):
        for cp in raw_copies(MUS[0], ahead, ahead):
            cp.start()

    lane = lax.broadcasted_iota(jnp.int32, (SUB, LANES), 1)
    sub = lax.broadcasted_iota(jnp.int32, (SUB, LANES), 0)
    zlane = lane % HALF
    zslot = ((lane + 3) % HALF) // SUB
    half1 = lane >= HALF

    def masks(i, carry):
        row = sub + i * SUB
        t_row = row // XH
        xh_i[rows8(i), :] = row - t_row * XH
        pz_i[rows8(i), :] = (t_row + zlane) % 2
        return carry
    lax.fori_loop(0, NV, masks, 0)

    def halo_copies(fi, c, kinds=range(4)):
        def mk(src, dst, kind, dev):
            return pltpu.make_async_remote_copy(src_ref=src, dst_ref=dst, send_sem=send_sem.at[fi, c, kind], recv_sem=recv_sem.at[fi, c, kind], device_id=dev, device_id_type=MESH)
        makers = (
            lambda: mk((fx.at[fi, 0, :, pl.ds(BASE, ROWS), :], pw.at[fi])[c], fy.at[fi, flip(c)], 0, (flip(yy), zz, tt)),
            lambda: mk(fx.at[fi, c, :, pl.ds(BASE, BASE), :], fx.at[fi, c, :, pl.ds(BASE + ROWS, BASE), :], 1, (yy, zz, t_prev)),
            lambda: mk(fx.at[fi, c, :, pl.ds(ROWS, BASE), :], fx.at[fi, c, :, pl.ds(0, BASE), :], 2, (yy, zz, t_next)),
            lambda: mk(zs.at[fi, c], zr.at[fi, c], 3, (yy, flip(zz), tt)),
        )
        return [makers[k]() for k in kinds]

    def start_halo(fi, c, kinds=range(4)):
        for cp in halo_copies(fi, c, kinds):
            cp.start()

    def wait_send(fi, c):
        for cp in halo_copies(fi, c):
            cp.wait_send()

    def wait_edges(fi, c):
        for cp in halo_copies(fi, c, (1, 2, 3)):
            cp.wait_recv()

    def wait_far(fi, c):
        halo_copies(fi, flip(c), (0,))[0].wait_recv()

    peers = []
    for d in range(1, DEVS):
        dev_y = flip(yy) if d // SUB else yy
        dev_z = flip(zz) if (d // 4) % 2 else zz
        dev_t = mod(tt + d % 4, 4)
        peers.append(((dev_y, dev_z, dev_t), dev_y * SUB + dev_z * 4 + mod(tt + 4 - d % 4, 4)))

    def red_copy(slot, d, src_dev):
        return pltpu.make_async_remote_copy(src_ref=red_own.at[slot], dst_ref=red.at[slot, src_dev], send_sem=rsend_sem.at[slot, d], recv_sem=rrecv_sem.at[slot, d], device_id=peers[d - 1][0], device_id_type=MESH)

    def red_start(slot, acc):
        red_own[slot] = acc
        for d in range(1, 16):
            red_copy(slot, d, me).start()

    def red_finish(slot):
        for d in range(1, 16):
            cp = red_copy(slot, d, peers[d - 1][1])
            cp.wait_send()
            cp.wait_recv()
        red[slot, me] = red_own[slot]
        total = red[slot, 0]
        for d in range(1, 16):
            total = total + red[slot, d]
        total = jnp.sum(jnp.sum(total, axis=0, keepdims=True), axis=1, keepdims=True)
        return jnp.broadcast_to(total, (SUB, LANES))

    def mat(par, c, slot, comp, rows):
        return g[par, c, slot * MATS + comp, rows, :]

    def adder(par, c, row, acc):
        def term(slot, vec):
            rows = pl.ds(row, SUB)
            for a in range(3):
                for b in range(3):
                    l_re = mat(par, c, slot, a * COLS + 2 * b, rows)
                    l_im = mat(par, c, slot, a * COLS + 2 * b + 1, rows)
                    v_re, v_im = vec[2 * b], vec[2 * b + 1]
                    for k, t in ((2 * a, l_re * v_re - l_im * v_im), (2 * a + 1, l_re * v_im + l_im * v_re)):
                        acc[k] = t if acc[k] is None else acc[k] + t
        return term

    def hop_own(par, c, i):
        fi = flip(par)
        row = pl.multiple_of(i * SUB, SUB)
        acc = [None] * COLS
        term = adder(par, c, row, acc)

        def ext(off):
            start = row + (BASE + off)
            return [fx[fi, c, k, pl.ds(start, SUB), :] for k in range(COLS)]

        own = ext(0)
        xh = xh_i[pl.ds(row, SUB), :]
        x_even = mod(pz_i[pl.ds(row, SUB), :] + c, 2) == par
        term(X0, own)
        lo, hi = ext(1), ext(-11)
        edge = xh == 11
        term(XP, [lax.select(edge, h, l) for l, h in zip(lo, hi)])
        lo, hi = ext(-1), ext(11)
        edge = xh == 0
        term(XM, [lax.select(edge, h, l) for l, h in zip(lo, hi)])
        m2, m2w, p2, p2w = ext(-2), ext(10), ext(2), ext(-10)
        low, high = xh < 2, xh > 9
        term(X2, [lax.select(x_even, lax.select(low, bw, bm), lax.select(high, fw, fp)) for bm, bw, fp, fw in zip(m2, m2w, p2, p2w)])
        mid = row + BASE
        loc = [fx[fi, flip(c), k, pl.ds(mid, SUB), :] for k in range(COLS)]
        term(LS, loc)
        term(LO, [pltpu.roll(v, HALF, 1) for v in loc])
        zpack = zr[fi, c, pl.ds(row, SUB), :]
        for slot, k in ((ZF1, NEAR), (ZF3, FAR)):
            edge = zlane >= HALF - k
            term(slot, [lax.select(edge, pltpu.roll(zpack, (HALF - k - SUB * j) % LANES, 1), pltpu.roll(own[j], LANES - k, 1)) for j in range(COLS)])
        for slot, k in ((ZB1, NEAR), (ZB3, FAR)):
            edge = zlane < k
            term(slot, [lax.select(edge, pltpu.roll(zpack, (k + HALF - SUB * j) % LANES, 1), pltpu.roll(own[j], k, 1)) for j in range(COLS)])
        term(TF1, ext(XH))
        term(TF3, ext(FAR * XH))
        term(TB1, ext(-XH))
        term(TB3, ext(-FAR * XH))
        return acc

    def hop(par, c):
        def body(i, carry):
            out = hop_own(par, c, i)
            for k in range(COLS):
                wv[k, rows8(i), :] = out[k]
            return carry
        lax.fori_loop(0, NV, body, 0)

    def across(par, c, i, vec, acc):
        term = adder(par, c, pl.multiple_of(i * SUB, SUB), acc)
        term(RS, vec)
        term(RO, [swap_halves(v) for v in vec])
        return acc

    def hop_far(par, c, i):
        rows = rows8(i)
        acc = [wv[k, rows, :] for k in range(COLS)]
        rem = [fy[flip(par), c, k, rows, :] for k in range(COLS)]
        if c == 0:
            return [a + v for a, v in zip(acc, rem)]
        return across(par, c, i, rem, acc)

    def sums_out(fi, i, vals):
        for k, v in enumerate(across(flip(fi), 0, i, vals, [None] * COLS)):
            pw[fi, k, rows8(i), :] = v

    in_slot = [zslot == j for j in range(COLS)]

    def zpack_of(vals):
        packed = vals[0]
        for j in range(1, COLS):
            packed = lax.select(in_slot[j], pltpu.roll(vals[j], SUB * j, 1), packed)
        return packed

    mass = jnp.full((SUB, LANES), mass_ref[0], F32)
    mass_sq = mass * mass
    zero = jnp.zeros((SUB, LANES), F32)

    def split_src(blk, carry):
        t, yp = half_of(blk), mod(blk, 2)
        c = yp
        for i in range(9):
            dn[0, SUB * i:SUB * i + SUB, :] = jnp.concatenate([src_ref[t, yp, SUB * i:SUB * i + SUB, :], src_ref[t, yp + 2, SUB * i:SUB * i + SUB, :]], axis=1)
        for k in range(COLS):
            fx[0, c, k, pl.ds(t * XH + BASE, SUB), :] = dn[0, pl.ds(k, SUB, stride=COLS), :]
            fx[0, c, k, pl.ds(t * XH + 48, 4), :] = dn[0, pl.ds(k + 48, 4, stride=COLS), :]
        return carry
    lax.fori_loop(0, XH, split_src, 0)

    acc = zero
    for c in range(2):
        def init_body(i, acc):
            rows, ext = rows8(i), rows8(i + 5)
            vals = [fx[0, c, k, ext, :] for k in range(COLS)]
            for k in range(COLS):
                fx[1, c, k, ext, :] = zero
                pv[c, k, rows, :] = zero
                xv[c, k, rows, :] = zero
                acc = acc + vals[k] * vals[k]
            zs[0, c, rows, :] = zpack_of(vals)
            return acc
        acc = lax.fori_loop(0, NV, init_body, acc)
        start_halo(0, c, range(c, 4))
    red_start(1, acc)

    c0, c1 = 0, 1
    sign = (-1.0, 1.0)
    comps = [(a * COLS + b * 2 + ri, b * COLS + a * 2 + ri, ri) for a in range(3) for b in range(3) for ri in range(2)]

    def densify(slot, wrap):
        def body(i, carry):
            for u in range(27):
                row = pl.multiple_of(i * (27 * SUB) + u * SUB, SUB)
                for typ in range(2):
                    dn[typ, pl.ds(row + ROWS, SUB), :] = jnp.concatenate([st[slot, typ, 0, pl.ds(row, SUB), :], st[slot, typ, 1, pl.ds(row, SUB), :]], axis=1)
            return carry
        lax.fori_loop(0, 2, body, 0)
        if wrap:
            for typ in range(2):
                dn[typ, :ROWS, :] = dn[typ, COLS * ROWS:, :]

    def base_of(slot):
        return slot * MATS

    def compact(order):
        mu = MUS[order]

        def block(blk, carry):
            slot = mod(blk, SLOTS)
            t, yp = half_of(blk), mod(blk, 2)
            c = yp
            ahead = blk + SLOTS - 1
            ahead_slot = mod(ahead, SLOTS)

            @pl.when(ahead < XH)
            def _():
                for cp in raw_copies(mu, ahead, ahead_slot):
                    cp.start()
            if order < 3:
                @pl.when(ahead >= XH)
                def _():
                    for cp in raw_copies(MUS[order + 1], ahead - XH, ahead_slot):
                        cp.start()
            for cp in raw_copies(mu, blk, slot):
                cp.wait()
            densify(slot, mu == 3)
            for off, n in ((0, SUB), (SUB, 4)):
                out_rows = pl.ds(t * XH + off, n)
                even = mod(zlane[:n] + (t + yp), 2) == 0

                def piece(typ, xpar, comp, back=0):
                    return dn[typ, pl.ds(ROWS + xpar * MATS + comp + STRIDE * (off - back), n, stride=STRIDE), :]

                def put(out_slot, comp, par, val):
                    g[par, c, base_of(out_slot) + comp, out_rows, :] = val
                for comp, adj, ri in comps:
                    if mu != 3:
                        for typ in range(2):
                            out_slot = out_slot_of(mu, typ, yp)
                            e, o = piece(typ, 0, comp), piece(typ, 1, comp)
                            put(out_slot, comp, 0, lax.select(even, e, o))
                            put(out_slot, comp, 1, lax.select(even, o, e))
                    else:
                        pairs = (
                            (X0, piece(0, 0, comp), sign[ri] * piece(0, 0, adj)),
                            (XP, piece(1, 0, comp), piece(0, 1, comp)),
                            (XM, sign[ri] * piece(0, 1, adj, 1), sign[ri] * piece(1, 0, adj, 1)),
                            (X2, sign[ri] * piece(1, 1, adj, 2), piece(1, 1, comp)),
                        )
                        for out_slot, e, o in pairs:
                            put(out_slot, comp, 0, lax.select(even, e, o))
                            put(out_slot, comp, 1, lax.select(even, o, e))
            return carry
        lax.fori_loop(0, XH, block, 0)

    def ly_copy():
        return pltpu.make_async_remote_copy(src_ref=y_out, dst_ref=y_in, send_sem=ly_send.at[0], recv_sem=ly_recv.at[0], device_id=(flip(yy), zz, tt), device_id_type=MESH)

    def lt_copies(par):
        dev = (yy, zz, t_next)
        out = []
        for c in range(2):
            out.append(pltpu.make_async_remote_copy(src_ref=g.at[flip(par), c, pl.ds(0, MATS), pl.ds(56, 16), :], dst_ref=tv_in.at[par, c], send_sem=lt_send.at[par, c, 0], recv_sem=lt_recv.at[par, c, 0], device_id=dev, device_id_type=MESH))
            out.append(pltpu.make_async_remote_copy(src_ref=g.at[flip(par), c, pl.ds(MATS, MATS), pl.ds(32, BASE), :], dst_ref=tw_in.at[par, c], send_sem=lt_send.at[par, c, 1], recv_sem=lt_recv.at[par, c, 1], device_id=dev, device_id_type=MESH))
        return out

    def lz_copy(par):
        return pltpu.make_async_remote_copy(src_ref=zl_out.at[par], dst_ref=zl_in.at[par], send_sem=lz_send.at[par], recv_sem=lz_recv.at[par], device_id=(yy, flip(zz), tt), device_id_type=MESH)

    compact(0)

    def y_pack(i, carry):
        rows = rows8(i)
        w0 = [swap_halves(mat(0, c0, RO, comp, rows)) for comp in range(MATS)]
        for comp in range(MATS):
            y_out[comp, rows, :] = lax.select(half1, mat(1, c0, RO, comp, rows), w0[comp])
        return carry
    lax.fori_loop(0, NV, y_pack, 0)
    ly_copy().start()

    compact(1)
    for par in (1, 0):
        for cp in lt_copies(par):
            cp.start()

    compact(2)

    def z_pack(n, carry):
        par, c = half_of(n), mod(n, 2)

        def body(i, carry):
            rows = rows8(i)
            for typ in range(2):
                for third in range(3):
                    zl_out[par, c, typ, third, rows, :] = zpack_of([mat(flip(par), c, ZF1 + typ, third * COLS + j, rows) for j in range(COLS)])
            return carry
        lax.fori_loop(0, NV, body, 0)
        return carry
    lax.fori_loop(0, 4, z_pack, 0)
    for par in (1, 0):
        lz_copy(par).start()

    def y_local(par, carry):
        def body(i, carry):
            rows = rows8(i)
            for src_c, own_c in ((c1, c0), (c0, c1)):
                far = [swap_halves(mat(flip(par), src_c, RO, adj, rows)) for comp, adj, ri in comps]
                own = [mat(par, own_c, RO, comp, rows) for comp in range(MATS)]
                for comp, adj, ri in comps:
                    g[par, own_c, LO * MATS + comp, rows, :] = lax.select(half1, sign[ri] * far[comp], own[comp])
            v0 = [mat(flip(par), c0, LS, adj, rows) for comp, adj, ri in comps]
            for comp, adj, ri in comps:
                g[par, c1, LS * MATS + comp, rows, :] = sign[ri] * v0[comp]
            return carry
        lax.fori_loop(0, NV, body, 0)
        return carry
    lax.fori_loop(0, 2, y_local, 0)

    def y_far(par):
        def body(i, carry):
            rows = rows8(i)
            w_in = [y_in[comp, rows, :] for comp in range(MATS)]
            if par == 0:
                w_in = [swap_halves(v) for v in w_in]
            v1 = [swap_halves(mat(flip(par), c1, RO, adj, rows)) for comp, adj, ri in comps]
            own = [mat(par, c1, RO, comp, rows) for comp in range(MATS)]
            for comp, adj, ri in comps:
                g[par, c1, RO * MATS + comp, rows, :] = lax.select(half1, own[comp], sign[ri] * w_in[adj])
                g[par, c0, RO * MATS + comp, rows, :] = lax.select(half1, w_in[comp], sign[ri] * v1[comp])
            w1 = [mat(flip(par), c1, RS, adj, rows) for comp, adj, ri in comps]
            for comp, adj, ri in comps:
                g[par, c0, RS * MATS + comp, rows, :] = sign[ri] * w1[comp]
            return carry
        lax.fori_loop(0, NV, body, 0)

    ly_copy().wait_send()
    ly_copy().wait_recv()
    y_far(1)

    def src_sums(i, carry):
        sums_out(0, i, [fx[0, 1, k, rows8(i + 5), :] for k in range(COLS)])
        return carry
    lax.fori_loop(0, NV, src_sums, 0)
    start_halo(0, 1, (0,))
    y_far(0)

    compact(3)

    for par in (1, 0):
        for cp in lt_copies(par):
            cp.wait_send()
            cp.wait_recv()

    def t_back(n, carry):
        par, c = half_of(n), mod(n, 2)

        def move(slot, dst, load, src):
            for off, cnt in ((0, SUB), (SUB, 4)):
                for comp, adj, ri in comps:
                    g[par, c, slot * MATS + comp, pl.ds(dst + off, cnt), :] = sign[ri] * load(adj, pl.ds(src + off, cnt))

        def v_local(q, carry):
            move(TB1, XH * q + XH, lambda k, rows: g[flip(par), c, k, rows, :], XH * q)
            return carry
        lax.fori_loop(0, 5, v_local, 0)
        move(TB1, 0, lambda k, rows: tv_in[par, c, k, rows, :], 4)

        def w_all(q, carry):
            move(TB3, XH * q + STRIDE, lambda k, rows: g[flip(par), c, MATS + k, rows, :], XH * q)
            move(TB3, XH * q, lambda k, rows: tw_in[par, c, k, rows, :], XH * q + 4)
            return carry
        lax.fori_loop(0, 3, w_all, 0)
        return carry
    lax.fori_loop(0, 4, t_back, 0)

    for par in (1, 0):
        lz_copy(par).wait_send()
        lz_copy(par).wait_recv()

    def z_back(n, carry):
        par, c = half_of(n), mod(n, 2)

        def body(i, carry):
            rows = rows8(i)
            for typ, k in ((0, NEAR), (1, FAR)):
                packs = [zl_in[par, c, typ, third, rows, :] for third in range(3)]
                back = []
                near_edge = zlane < k
                for comp, adj, ri in comps:
                    own = pltpu.roll(mat(flip(par), c, 4 + typ, adj, rows), k, 1)
                    far = pltpu.roll(packs[adj // COLS], (k + HALF - SUB * (adj % COLS)) % LANES, 1)
                    back.append(sign[ri] * lax.select(near_edge, far, own))
                for comp, val in enumerate(back):
                    g[par, c, (COLS + typ) * MATS + comp, rows, :] = val
            return carry
        lax.fori_loop(0, NV, body, 0)
        return carry
    lax.fori_loop(0, 4, z_back, 0)


    rho0 = red_finish(1)
    scal[0] = rho0
    scal[1] = rho0
    scal[2] = zero

    def cg_step(step, carry):
        def odd_group(c, acc):
            wait_edges(0, c)
            hop(1, c)

            @pl.when(step > 0)
            def _():
                wait_send(1, c)
            wait_far(0, c)

            if c == 0:
                @pl.when(step > 0)
                def _():
                    rho = red_finish(1)
                    norm_ref[pl.ds(step - 1, 1), :] = (rho / scal[0])[0:1]
                    scal[2] = rho / scal[1]
                    scal[1] = rho
            beta = scal[2]

            def body(n, acc):
                packs = []
                for u in range(3):
                    i = n * 3 + u
                    rows, ext = rows8(i), rows8(i + 5)
                    vals = hop_far(1, c, i)
                    for k in range(COLS):
                        s_new = vals[k] + beta * fx[1, c, k, ext, :]
                        p_new = fx[0, c, k, ext, :] + beta * pv[c, k, rows, :]
                        fx[1, c, k, ext, :] = s_new
                        pv[c, k, rows, :] = p_new
                        acc = acc + (s_new * s_new + mass_sq * (p_new * p_new))
                        vals[k] = s_new
                    packs.append((rows, zpack_of(vals)))
                    if c == 1:
                        sums_out(1, i, vals)
                for rows, pack in packs:
                    zs[1, c, rows, :] = pack
                return acc
            acc = lax.fori_loop(0, 3, body, acc)

            if c == 1:
                red_start(0, acc)
            start_halo(1, c)
            return acc
        odd_group(1, odd_group(0, zero))

        def even_group(c, acc):
            wait_edges(1, c)
            hop(0, c)
            wait_send(0, c)
            wait_far(1, c)

            if c == 1:
                scal[3] = scal[1] / red_finish(0)
            alpha = scal[3]

            def body(n, acc):
                packs = []
                for u in range(3):
                    i = n * 3 + u
                    rows, ext = rows8(i), rows8(i + 5)
                    vals = hop_far(0, c, i)
                    for k in range(COLS):
                        p_val = pv[c, k, rows, :]
                        q_val = mass_sq * p_val - vals[k]
                        xv[c, k, rows, :] = xv[c, k, rows, :] + alpha * p_val
                        r_new = fx[0, c, k, ext, :] - alpha * q_val
                        fx[0, c, k, ext, :] = r_new
                        acc = acc + r_new * r_new
                        vals[k] = r_new
                    packs.append((rows, zpack_of(vals)))
                    if c == 1:
                        sums_out(0, i, vals)
                for rows, pack in packs:
                    zs[0, c, rows, :] = pack
                return acc
            acc = lax.fori_loop(0, 3, body, acc)

            if c == 0:
                red_start(1, acc)

            @pl.when(step < ITERS - 1)
            def _():
                start_halo(0, c)
            return acc
        even_group(0, even_group(1, zero))
        return carry
    lax.fori_loop(0, ITERS, cg_step, 0)

    for c in range(2):
        wait_send(1, c)

    def join_sol(blk, carry):
        t, yp = half_of(blk), mod(blk, 2)
        c = yp
        for k in range(COLS):
            dn[0, pl.ds(k, SUB, stride=COLS), :] = xv[c, k, pl.ds(t * XH, SUB), :]
            dn[0, pl.ds(k + 48, 4, stride=COLS), :] = xv[c, k, pl.ds(t * XH + SUB, 4), :]
        for i in range(9):
            val = dn[0, SUB * i:SUB * i + SUB, :]
            sol_ref[t, yp, SUB * i:SUB * i + SUB, :] = val[:, :HALF]
            sol_ref[t, yp + 2, SUB * i:SUB * i + SUB, :] = pltpu.roll(val, HALF, 1)[:, :HALF]
        return carry
    lax.fori_loop(0, XH, join_sol, 0)
    rho = red_finish(1)
    norm_ref[pl.ds(ITERS - 1, 1), :] = (rho / scal[0])[0:1]


def solution(mesh):
    link_spec = P(None, *CUTS)
    field_spec = P(*CUTS)
    vmem = pl.BlockSpec(memory_space=pltpu.VMEM)

    def local_solve(fat_links, long_links, source, quark_mass):
        t_len, z_len, y_len, xh_len = source.shape[:4]

        def link_rows(links):
            return jnp.moveaxis(links, 2, -1).reshape(4, t_len, y_len, STRIDE * xh_len, z_len)
        src = jnp.moveaxis(source, 1, -1).reshape(t_len, y_len, COLS * xh_len, z_len)
        hbm = pl.BlockSpec(memory_space=pl.ANY)
        dma = pltpu.SemaphoreType.DMA
        sol, norms = pl.pallas_call(
            cg_kernel,
            out_shape=(jax.ShapeDtypeStruct(src.shape, F32), jax.ShapeDtypeStruct((SUB, LANES), F32)),
            in_specs=[vmem, pl.BlockSpec(memory_space=pltpu.SMEM), hbm, hbm],
            out_specs=(vmem, vmem),
            scratch_shapes=[
                pltpu.VMEM(PP + (288, ROWS, LANES), F32),
                pltpu.VMEM(PP + (COLS, EXT, LANES), F32),
                pltpu.VMEM(PP + (COLS, ROWS, LANES), F32),
                pltpu.VMEM(PP + (ROWS, LANES), F32),
                pltpu.VMEM(PP + (ROWS, LANES), F32),
                pltpu.VMEM((2, COLS, ROWS, LANES), F32),
                pltpu.VMEM((2, COLS, ROWS, LANES), F32),
                pltpu.VMEM((COLS, ROWS, LANES), F32),
                pltpu.VMEM((ROWS, LANES), jnp.int32),
                pltpu.VMEM((ROWS, LANES), jnp.int32),
                pltpu.VMEM((2, SUB, LANES), F32),
                pltpu.VMEM((2, 16, SUB, LANES), F32),
                pltpu.VMEM((4, SUB, LANES), F32),
                pltpu.VMEM((SLOTS, 2, 2, STRIDE * xh_len, z_len), F32),
                pltpu.VMEM((2, 504, LANES), F32),
                pltpu.VMEM((2, COLS, ROWS, LANES), F32),
                pltpu.VMEM((MATS, ROWS, LANES), F32),
                pltpu.VMEM((MATS, ROWS, LANES), F32),
                pltpu.VMEM(PP + (MATS, 16, LANES), F32),
                pltpu.VMEM(PP + (MATS, BASE, LANES), F32),
                pltpu.VMEM(PP + (2, 3, ROWS, LANES), F32),
                pltpu.VMEM(PP + (2, 3, ROWS, LANES), F32),
                *[dma(n) for n in ((SLOTS, 2, 2), (1,), (1,), PP + (2,), PP + (2,))], dma((2,)), dma((2,)),
                dma(PP + (4,)), dma(PP + (4,)), dma((2, DEVS)), dma((2, DEVS)),
            ],
            compiler_params=pltpu.CompilerParams(has_side_effects=True, vmem_limit_bytes=61 * 1024 * 1024),
        )(src, quark_mass, link_rows(fat_links), link_rows(long_links))
        sol = jnp.moveaxis(sol.reshape(t_len, y_len, xh_len, 3, 2, z_len), -1, 1)
        return sol, norms[:, 0]

    return jax.shard_map(local_solve, mesh=mesh, in_specs=(link_spec, link_spec, field_spec, P()), out_specs=(field_spec, P()), check_vma=False)
```

time: 252 us -> 225 us (0.89)
  Pallas kernels: 246 us -> 219 us
    pallas_call x1, Pallas kernels: 246 us -> 219 us  [local_solve(): pl.pallas_call(cg_kernel, out_shape=(jax.ShapeDtypeStruct(src.shape, F32)...]
where the time goes in v1:
time: 225 us; the launch traced here: 224 us
  Pallas kernels  219 us (97%)
  local copies, waits for them, and re-layouts  3.69 us (2%)
    pallas_call x1, Pallas kernels, local_solve(): pl.pallas_call(cg_kernel, out_shape=(jax.ShapeDtypeStruct(src.shape, F32)...  219 us

profile of v1, /device:TPU:0, one launch (start us, length us, event | category | flops | bytes accessed | tf_op | source)
XLA Modules:
  0.0 224.4 jit_solution(18260980396843696585)
XLA Ops:
  1.3 219.4 %shard_map.59 = (f32[6,4,72,64]{3,2,1,0:T(8,128)}, f32[8,128]{1,0:T(8,128)}) custom-call(f32[6,4,72,64]{3,2,1,0:T(8,128)} %bitcast.14, f32[1]{0:T(128)S(6)} %copy.7.mass_ref, f32[4,6,4,432,64]{4,3,2,1,0:T(8,128)} %bitcast.12, f32[4,6,4,432,64]{4,3,2,1,0:T(8,128)} %bitcast.13), custom_call_target="tpu_custom_call" | custom-call | tf_op jit(solution)/shard_map/pallas_call | solution.py:613
  220.7 1.3 slice_reduce_fusion
  222.0 2.4 %copy.8 = f32[6,64,4,12,3,2]{1,5,4,3,2,0:T(2,128)} copy(f32[6,64,4,12,3,2]{1,5,4,3,2,0:T(2,128)} %bitcast.15) | data formatting | bytes 884736

commit v2 on v1

--- a/solution.py
+++ b/solution.py
@@ -432,67 +432,60 @@
 
     compact(3)
 
-    for par in (1, 0):
-        for cp in lt_copies(par):
+    def derive(par):
+        for cp in lt_copies(par) + [lz_copy(par)]:
             cp.wait_send()
             cp.wait_recv()
 
-    def t_back(n, carry):
-        par, c = half_of(n), mod(n, 2)
-
-        def move(slot, dst, load, src):
-            for off, cnt in ((0, SUB), (SUB, 4)):
-                for comp, adj, ri in comps:
-                    g[par, c, slot * MATS + comp, pl.ds(dst + off, cnt), :] = sign[ri] * load(adj, pl.ds(src + off, cnt))
-
-        def v_local(q, carry):
-            move(TB1, XH * q + XH, lambda k, rows: g[flip(par), c, k, rows, :], XH * q)
-            return carry
-        lax.fori_loop(0, 5, v_local, 0)
-        move(TB1, 0, lambda k, rows: tv_in[par, c, k, rows, :], 4)
-
-        def w_all(q, carry):
-            move(TB3, XH * q + STRIDE, lambda k, rows: g[flip(par), c, MATS + k, rows, :], XH * q)
-            move(TB3, XH * q, lambda k, rows: tw_in[par, c, k, rows, :], XH * q + 4)
-            return carry
-        lax.fori_loop(0, 3, w_all, 0)
-        return carry
-    lax.fori_loop(0, 4, t_back, 0)
-
-    for par in (1, 0):
-        lz_copy(par).wait_send()
-        lz_copy(par).wait_recv()
-
-    def z_back(n, carry):
-        par, c = half_of(n), mod(n, 2)
-
-        def body(i, carry):
-            rows = rows8(i)
-            for typ, k in ((0, NEAR), (1, FAR)):
-                packs = [zl_in[par, c, typ, third, rows, :] for third in range(3)]
-                back = []
-                near_edge = zlane < k
-                for comp, adj, ri in comps:
-                    own = pltpu.roll(mat(flip(par), c, 4 + typ, adj, rows), k, 1)
-                    far = pltpu.roll(packs[adj // COLS], (k + HALF - SUB * (adj % COLS)) % LANES, 1)
-                    back.append(sign[ri] * lax.select(near_edge, far, own))
-                for comp, val in enumerate(back):
-                    g[par, c, (COLS + typ) * MATS + comp, rows, :] = val
-            return carry
-        lax.fori_loop(0, NV, body, 0)
-        return carry
-    lax.fori_loop(0, 4, z_back, 0)
-
-
+        def t_back(c, carry):
+
+            def move(slot, dst, load, src):
+                for off, cnt in ((0, SUB), (SUB, 4)):
+                    for comp, adj, ri in comps:
+                        g[par, c, slot * MATS + comp, pl.ds(dst + off, cnt), :] = sign[ri] * load(adj, pl.ds(src + off, cnt))
+
+            def v_local(q, carry):
+                move(TB1, XH * q + XH, lambda k, rows: g[flip(par), c, k, rows, :], XH * q)
+                return carry
+            lax.fori_loop(0, 5, v_local, 0)
+            move(TB1, 0, lambda k, rows: tv_in[par, c, k, rows, :], 4)
+
+            def w_all(q, carry):
+                move(TB3, XH * q + STRIDE, lambda k, rows: g[flip(par), c, MATS + k, rows, :], XH * q)
+                move(TB3, XH * q, lambda k, rows: tw_in[par, c, k, rows, :], XH * q + 4)
+                return carry
+            lax.fori_loop(0, 3, w_all, 0)
+            return carry
+        lax.fori_loop(0, 2, t_back, 0)
+
+        def z_back(c, carry):
+
+            def body(i, carry):
+                rows = rows8(i)
+                for typ, k in ((0, NEAR), (1, FAR)):
+                    packs = [zl_in[par, c, typ, third, rows, :] for third in range(3)]
+                    back = []
+                    near_edge = zlane < k
+                    for comp, adj, ri in comps:
+                        own = pltpu.roll(mat(flip(par), c, 4 + typ, adj, rows), k, 1)
+                        far = pltpu.roll(packs[adj // COLS], (k + HALF - SUB * (adj % COLS)) % LANES, 1)
+                        back.append(sign[ri] * lax.select(near_edge, far, own))
+                    for comp, val in enumerate(back):
+                        g[par, c, (COLS + typ) * MATS + comp, rows, :] = val
+                return carry
+            lax.fori_loop(0, NV, body, 0)
+            return carry
+        lax.fori_loop(0, 2, z_back, 0)
+
+    derive(1)
     rho0 = red_finish(1)
     scal[0] = rho0
     scal[1] = rho0
     scal[2] = zero
 
     def cg_step(step, carry):
-        def odd_group(c, acc):
-            wait_edges(0, c)
-            hop(1, c)
+        def odd_group(c):
+            acc = zero if c == 0 else scal[4]
 
             @pl.when(step > 0)
             def _():
@@ -531,13 +524,24 @@
 
             if c == 1:
                 red_start(0, acc)
+            else:
+                scal[4] = acc
             start_halo(1, c)
-            return acc
-        odd_group(1, odd_group(0, zero))
-
-        def even_group(c, acc):
-            wait_edges(1, c)
-            hop(0, c)
+
+        def odd_pass(c, carry):
+            wait_edges(0, c)
+            hop(1, c)
+            pl.when(c == 0)(lambda: odd_group(0))
+            pl.when(c == 1)(lambda: odd_group(1))
+            return carry
+        lax.fori_loop(0, 2, odd_pass, 0)
+
+        @pl.when(step == 0)
+        def _():
+            derive(0)
+
+        def even_group(c):
+            acc = zero if c == 1 else scal[4]
             wait_send(0, c)
             wait_far(1, c)
 
@@ -569,12 +573,21 @@
 
             if c == 0:
                 red_start(1, acc)
+            else:
+                scal[4] = acc
 
             @pl.when(step < ITERS - 1)
             def _():
                 start_halo(0, c)
-            return acc
-        even_group(0, even_group(1, zero))
+
+        def even_pass(n, carry):
+            c = flip(n)
+            wait_edges(1, c)
+            hop(0, c)
+            pl.when(c == 1)(lambda: even_group(1))
+            pl.when(c == 0)(lambda: even_group(0))
+            return carry
+        lax.fori_loop(0, 2, even_pass, 0)
         return carry
     lax.fori_loop(0, ITERS, cg_step, 0)
 
@@ -628,7 +641,7 @@
                 pltpu.VMEM((ROWS, LANES), jnp.int32),
                 pltpu.VMEM((2, SUB, LANES), F32),
                 pltpu.VMEM((2, 16, SUB, LANES), F32),
-                pltpu.VMEM((4, SUB, LANES), F32),
+                pltpu.VMEM((5, SUB, LANES), F32),
                 pltpu.VMEM((SLOTS, 2, 2, STRIDE * xh_len, z_len), F32),
                 pltpu.VMEM((2, 504, LANES), F32),
                 pltpu.VMEM((2, COLS, ROWS, LANES), F32),

time: 225 us -> 211 us (0.938)
  Pallas kernels: 219 us -> 205 us
    pallas_call x1, Pallas kernels: 219 us -> 205 us  [local_solve(): pl.pallas_call(cg_kernel, out_shape=(jax.ShapeDtypeStruct(src.shape, F32)...]
where the time goes in v2:
time: 211 us; the launch traced here: 210 us
  Pallas kernels  205 us (97%)
  local copies, waits for them, and re-layouts  3.69 us (2%)
    pallas_call x1, Pallas kernels, local_solve(): pl.pallas_call(cg_kernel, out_shape=(jax.ShapeDtypeStruct(src.shape, F32)...  205 us

profile of v2, /device:TPU:0, one launch (start us, length us, event | category | flops | bytes accessed | tf_op | source)
XLA Modules:
  0.0 210.4 jit_solution(15582697992516265632)
XLA Ops:
  1.3 205.5 %shard_map.59 = (f32[6,4,72,64]{3,2,1,0:T(8,128)}, f32[8,128]{1,0:T(8,128)}) custom-call(f32[6,4,72,64]{3,2,1,0:T(8,128)} %bitcast.14, f32[1]{0:T(128)S(6)} %copy.7.mass_ref, f32[4,6,4,432,64]{4,3,2,1,0:T(8,128)} %bitcast.12, f32[4,6,4,432,64]{4,3,2,1,0:T(8,128)} %bitcast.13), custom_call_target="tpu_custom_call" | custom-call | tf_op jit(solution)/shard_map/pallas_call | solution.py:626
  206.8 1.3 slice_reduce_fusion
  208.1 2.4 %copy.8 = f32[6,64,4,12,3,2]{1,5,4,3,2,0:T(2,128)} copy(f32[6,64,4,12,3,2]{1,5,4,3,2,0:T(2,128)} %bitcast.15) | data formatting | bytes 884736

commit v3 on v2

--- a/solution.py
+++ b/solution.py
@@ -20,7 +20,7 @@
 STRIDE = 36
 DEVS = 16
 NEAR, FAR = 1, 3
-SLOTS = 4
+SLOTS = 6
 PP = (2, 2)
 CUTS = ('t', 'zz', 'yy')
 COLS = 6

time: 211 us -> 210 us (level)
  no operation moved by 1% of the time
where the time goes in v3:
time: 210 us; the launch traced here: 209 us
  Pallas kernels  204 us (97%)
  local copies, waits for them, and re-layouts  3.69 us (2%)
    pallas_call x1, Pallas kernels, local_solve(): pl.pallas_call(cg_kernel, out_shape=(jax.ShapeDtypeStruct(src.shape, F32)...  204 us

profile of v3, /device:TPU:0, one launch (start us, length us, event | category | flops | bytes accessed | tf_op | source)
XLA Modules:
  0.0 209.4 jit_solution(6548398843261586644)
XLA Ops:
  1.3 204.4 %shard_map.59 = (f32[6,4,72,64]{3,2,1,0:T(8,128)}, f32[8,128]{1,0:T(8,128)}) custom-call(f32[6,4,72,64]{3,2,1,0:T(8,128)} %bitcast.14, f32[1]{0:T(128)S(6)} %copy.7.mass_ref, f32[4,6,4,432,64]{4,3,2,1,0:T(8,128)} %bitcast.12, f32[4,6,4,432,64]{4,3,2,1,0:T(8,128)} %bitcast.13), custom_call_target="tpu_custom_call" | custom-call | tf_op jit(solution)/shard_map/pallas_call | solution.py:626
  205.7 1.3 slice_reduce_fusion
  207.0 2.4 %copy.8 = f32[6,64,4,12,3,2]{1,5,4,3,2,0:T(2,128)} copy(f32[6,64,4,12,3,2]{1,5,4,3,2,0:T(2,128)} %bitcast.15) | data formatting | bytes 884736
